TPU v7x, 32 devices: a whole 2x2x4 slice. The times are simulated.
32 devices in a mesh: dp: 2 (over x), tp: 4 (over z), sp: 4 (over y, core).
Axes of the slice: x: 2, y: 2, z: 4, core: 2. Of those that a mesh axis runs over, the one named last changes fastest.
Arguments:
- hidden: bfloat16 [128, 8192], P('dp'), parts along dimension 0
- seq_lens: int32 [128], P('dp'), parts along dimension 0
- rope_cos: float32 [128, 64], P('dp'), parts along dimension 0
- rope_sin: float32 [128, 64], P('dp'), parts along dimension 0
- k_cache: bfloat16 [128, 256, 8, 128], P('dp', 'sp', 'tp'), parts along dimension 0
- v_cache: bfloat16 [128, 256, 8, 128], P('dp', 'sp', 'tp'), parts along dimension 0
- norm_gain: bfloat16 [8192], replicated
- w_qkv: bfloat16 [8192, 8, 1280], P(None, 'tp')
- b_qkv: bfloat16 [8, 1280], P('tp')
- sink_logits: float32 [64], P('tp')
- w_o: bfloat16 [8192, 8192], P('tp')
- b_o: bfloat16 [8192], replicated
Outputs:
- output 1: bfloat16 [128, 8192], P('dp'), parts along dimension 0
- output 2: bfloat16 [128, 256, 8, 128], P('dp', 'sp', 'tp'), parts along dimension 0
- output 3: bfloat16 [128, 256, 8, 128], P('dp', 'sp', 'tp'), parts along dimension 0
There are 2 independent parts. A program takes and returns all parts, laid end to end along the dimension named above; an argument that names none is the same for every part.
All inputs are finite; a program needn't handle non-finite values.
Results may differ from a plain program's by a relative error of at most 0.00542463.
Values sent between devices are 32-bit elements.
A program may use at most 1 GiB of HBM per device.

v0:
```python
import jax
import jax.numpy as jnp
from jax import lax
from jax.sharding import PartitionSpec as P

NORM_EPS = 1e-5


def rotate_half(heads_in, cos_part, sin_part):
    half_dim = heads_in.shape[-1] // 2
    first_half = heads_in[..., :half_dim]
    second_half = heads_in[..., half_dim:]
    return jnp.concatenate([first_half * cos_part - second_half * sin_part, second_half * cos_part + first_half * sin_part], axis=-1)


def local_partials(hidden, seq_lens, rope_cos, rope_sin, k_cache, v_cache, norm_gain, w_qkv, b_qkv, sink_logits):
    num_seqs, ctx_local, kv_local, head_dim = k_cache.shape
    group_size = w_qkv.shape[2] // head_dim - 2
    x_wide = hidden.astype(jnp.float32)
    inv_rms = lax.rsqrt(jnp.mean(x_wide * x_wide, axis=-1, keepdims=True) + NORM_EPS)
    normed = (x_wide * inv_rms * norm_gain.astype(jnp.float32)).astype(jnp.bfloat16)
    qkv_all = jnp.einsum("bd,dkc->bkc", normed, w_qkv, preferred_element_type=jnp.float32) + b_qkv.astype(jnp.float32)
    qkv_all = qkv_all.reshape(num_seqs, kv_local, group_size + 2, head_dim)
    q_rot = rotate_half(qkv_all[:, :, :group_size], rope_cos[:, None, None, :], rope_sin[:, None, None, :]).astype(jnp.bfloat16)
    k_new = rotate_half(qkv_all[:, :, group_size], rope_cos[:, None, :], rope_sin[:, None, :]).astype(jnp.bfloat16)
    v_new = qkv_all[:, :, group_size + 1].astype(jnp.bfloat16)
    positions = lax.axis_index("sp") * ctx_local + jnp.arange(ctx_local)
    is_new = (positions[None, :] == seq_lens[:, None])[:, :, None, None]
    k_out = jnp.where(is_new, k_new[:, None], k_cache)
    v_out = jnp.where(is_new, v_new[:, None], v_cache)
    logits = jnp.einsum("bkgd,blkd->bkgl", q_rot, k_out, preferred_element_type=jnp.float32) * head_dim ** -0.5
    logits = jnp.where((positions[None, :] <= seq_lens[:, None])[:, None, None, :], logits, -jnp.inf)
    row_max = jnp.maximum(jnp.max(logits, axis=-1), sink_logits.reshape(kv_local, group_size))
    weights = jnp.exp(logits - row_max[..., None])
    row_sum = jnp.sum(weights, axis=-1)
    weighted = jnp.einsum("bkgl,blkd->bkgd", weights.astype(jnp.bfloat16), v_out, preferred_element_type=jnp.float32)
    packed = jnp.concatenate([row_max[..., None], row_sum[..., None], weighted], axis=-1)
    return packed.reshape(num_seqs, kv_local * group_size, head_dim + 2), k_out, v_out


def combine_shards(parts_in, sinks_here):
    shard_max = parts_in[..., 0]
    shard_sum = parts_in[..., 1]
    top_max = jnp.max(shard_max, axis=1)
    rescale = jnp.exp(shard_max - top_max[:, None])
    denominator = jnp.sum(shard_sum * rescale, axis=1) + jnp.exp(sinks_here[None, :] - top_max)
    combined = jnp.sum(parts_in[..., 2:] * rescale[..., None], axis=1)
    return combined / denominator[..., None]


def solution(mesh):
    sp_size = mesh.shape["sp"]
    cache_spec = P("dp", "sp", "tp", None)

    def block_step(hidden, seq_lens, rope_cos, rope_sin, k_cache, v_cache, norm_gain, w_qkv, b_qkv, sink_logits, w_o, b_o):
        packed, k_out, v_out = local_partials(hidden, seq_lens, rope_cos, rope_sin, k_cache, v_cache, norm_gain, w_qkv, b_qkv, sink_logits)
        num_seqs, local_heads, width = packed.shape
        head_dim = width - 2
        head_share = local_heads // sp_size
        received = lax.all_to_all(packed.reshape(num_seqs, sp_size, head_share, width), "sp", 1, 1, tiled=True)
        sp_index = lax.axis_index("sp")
        sinks_here = sink_logits.reshape(sp_size, head_share)[sp_index]
        combined = combine_shards(received, sinks_here)
        w_rows = w_o.reshape(sp_size, head_share * head_dim, w_o.shape[1])[sp_index]
        partial_out = jnp.dot(combined.astype(jnp.bfloat16).reshape(num_seqs, head_share * head_dim), w_rows, preferred_element_type=jnp.float32)
        summed = lax.psum(partial_out, ("tp", "sp"))
        out_hidden = (hidden.astype(jnp.float32) + summed + b_o.astype(jnp.float32)).astype(jnp.bfloat16)
        return out_hidden, k_out, v_out

    return jax.shard_map(block_step, mesh=mesh, in_specs=(P("dp", None), P("dp"), P("dp", None), P("dp", None), cache_spec, cache_spec, P(None), P(None, "tp", None), P("tp", None), P("tp"), P("tp", None), P(None)), out_specs=(P("dp", None), cache_spec, cache_spec), check_vma=False)
```

profile of v0, /device:TPU:0, one launch (start us, length us, event | category | flops | bytes accessed | tf_op | source)
XLA Modules:
  0.0 178.9 jit_solution(5883238684445538941)
XLA Ops:
  7.2 0.7 convert_element_type.50
  7.9 0.7 convert_element_type.52
  8.6 1.5 fusion.8
  10.1 18.4 %fusion.5 = f32[64,2,1280]{2,0,1:T(8,128)S(1)} fusion(bf16[8192,2,1280]{2,1,0:T(2,128)(2,1)} %param.19, bf16[64,8192]{1,0:T(8,128)(2,1)} %param.12, f32[8192]{0:T(1024)S(1)} %convert_element_type.50, f32[64]{0:T(128)S(1)} %add_rsqrt_fusion, f32[2,1280]{1,0:T(2,128)S(1)} %convert_element_type.52), kind=kOutput, calls=%fused_computation.10 | convolution fusion | flops 2686615552 | bytes 43690240 | tf_op jit(solution)/shard_map/bd,dkc->bkc/dot_general | solution.py:22
  28.6 0.1 reshape.156
  28.8 0.2 fusion.43
  29.0 0.2 copy-done.5
  29.2 0.1 max.30
  29.3 0.1 max.27
  29.4 0.1 subtract_convert_fusion.1
  29.5 0.1 pad_maximum_fusion.1
  29.7 0.1 broadcast_compare_fusion.1
  29.8 0.1 subtract_convert_fusion
  29.9 7.9 %broadcast_select_fusion.1 = (bf16[64,64,2,128]{3,2,1,0:T(2,128)(2,1)S(1)}, bf16[64,64,2,128]{3,2,1,0:T(2,128)(2,1)}) fusion(bf16[64,64,2,128]{3,2,1,0:T(2,128)(2,1)} %param.16, pred[64,64]{1,0:T(8,128)(4,1)S(1)} %get-tuple-element.15, bf16[64,2,128]{2,1,0:T(2,128)(2,1)S(1)} %copy.68, bf16[64,64,2,128]{3,2,1,0:T(2,128)(2,1)} %param.17, ...), kind=kLoop, calls=%fused_computation.6 | loop fusion | flops 2097152 | bytes 8458240 | tf_op jit(solution)/shard_map/jit(_where)/select_n | solution.py:29
  37.8 1.4 fusion.44
  39.3 0.4 fusion.29
  39.7 2.3 %fusion.13 = f32[64,2,8,128]{3,2,1,0:T(8,128)S(1)} fusion(bf16[64,64,2,128]{3,2,1,0:T(2,128)(2,1)} %get-tuple-element.13, f32[64,2,8,64]{3,2,1,0:T(8,128)S(1)} %get-tuple-element.17, f32[64,2,8]{2,1,0:T(2,128)S(1)} %bitcast.43), kind=kOutput, calls=%fused_computation.16 | convolution fusion | flops 16908288 | bytes 2887680 | tf_op jit(solution)/shard_map/bkgl,blkd->bkgd/dot_general | solution.py:36
  42.0 0.2 copy.76
  42.3 0.2 copy.75
  42.6 0.1 broadcast_maximum_fusion.1
  42.6 0.2 copy.74
  42.9 1.6 pad_maximum_fusion
  44.5 4.3 %all-to-all-start = ((f32[64,4,4,130]{3,0,2,1:T(8,128)}), f32[64,4,4,130]{3,0,2,1:T(8,128)S(1)}, u32[]{:S(2)}, u32[]{:S(2)}) async-start(f32[64,4,4,130]{3,0,2,1:T(8,128)} %pad_maximum_fusion), calls=%async_computation | async-start | bytes 2097152 | tf_op jit(solution)/shard_map/all_to_all | solution.py:60
  48.8 14.2 %all-to-all-done = f32[64,4,4,130]{3,0,2,1:T(8,128)S(1)} async-done(((f32[64,4,4,130]{3,0,2,1:T(8,128)}), f32[64,4,4,130]{3,0,2,1:T(8,128)S(1)}, u32[]{:S(2)}, u32[]{:S(2)}) %all-to-all-start) | async-done | bytes 532512 | tf_op jit(solution)/shard_map/all_to_all | solution.py:60
  63.0 0.4 slice_reduce_fusion
  63.4 0.2 copy.85
  63.7 0.1 exponential_add_fusion
  63.8 0.3 fusion.27
  64.1 6.3 %fusion.2 = f32[64,8192]{1,0:T(8,128)} fusion(bf16[4,512,8192]{2,1,0:T(8,128)(2,1)} %bitcast.38, s32[]{:T(128)S(6)} %select_n.18, f32[64,4,128]{2,0,1:T(8,128)S(1)} %fusion.27, f32[64,4]{0,1:T(4,128)S(1)} %exponential_add_fusion), kind=kOutput, calls=%fused_computation.2 | convolution fusion | flops 536936448 | bytes 10617860 | tf_op jit(solution)/shard_map/dot_general | solution.py:65
  70.5 0.7 copy-done.4
  71.1 98.1 %all-reduce.2.cloned.1.call-done = f32[64,8192]{1,0:T(8,128)} async-done(((f32[64,8192]{1,0:T(8,128)}), f32[64,8192]{1,0:T(8,128)}) %all-reduce.2.cloned.1.call-update) | async-done | bytes 2097168 | tf_op jit(solution)/shard_map/psum | solution.py:66
  169.2 2.8 %fusion.12 = bf16[64,8192]{1,0:T(8,128)(2,1)} fusion(f32[64,8192]{1,0:T(8,128)} %all-reduce.2.cloned.1.call-done, bf16[64,8192]{1,0:T(8,128)(2,1)S(1)} %copy-done.1, f32[8192]{0:T(1024)S(1)} %convert_element_type.57), kind=kLoop, calls=%fused_computation.15 | loop fusion | flops 2097152 | bytes 4227072 | tf_op jit(solution)/shard_map/convert_element_type | solution.py:67
  (28 shorter events, 0.5 us)
Async XLA Ops:
  28.6 0.7 copy-start.5
  28.6 0.8 copy-start.2
  28.6 0.8 copy-start.3
  28.6 1.1 copy-start.6
  37.8 4.2 %copy-start = (bf16[64,64,2,128]{3,2,1,0:T(2,128)(2,1)}, bf16[64,64,2,128]{3,2,1,0:T(2,128)(2,1)S(1)}, u32[]{:S(2)}) copy-start(bf16[64,64,2,128]{3,2,1,0:T(2,128)(2,1)S(1)} %get-tuple-element.12) | copy-start | bytes 6291460
  44.5 18.5 %all-to-all-start = ((f32[64,4,4,130]{3,0,2,1:T(8,128)}), f32[64,4,4,130]{3,0,2,1:T(8,128)S(1)}, u32[]{:S(2)}, u32[]{:S(2)}) async-start(f32[64,4,4,130]{3,0,2,1:T(8,128)} %pad_maximum_fusion), calls=%async_computation | async-start | bytes 2097152 | tf_op jit(solution)/shard_map/all_to_all | solution.py:60
  48.8 120.5 %all-reduce.2.cloned.1.call-start = ((), (), s32[]{:S(2)}) async-start(), calls=%async_computation.1 | async-start | bytes 4194304 | tf_op jit(solution)/shard_map/psum | solution.py:66
  70.4 0.7 copy-start.4
  70.4 98.8 %copy-start.1 = (bf16[64,8192]{1,0:T(8,128)(2,1)S(1)}, bf16[64,8192]{1,0:T(8,128)(2,1)}, u32[]{:S(2)}) copy-start(bf16[64,8192]{1,0:T(8,128)(2,1)} %param.12) | copy-start | bytes 3145732
Sparse Core Ops, SparseCore 0:
  70.6 98.5 all-reduce.1
where the time goes:
time: 179 us
  waiting for transfers between devices  112 us (63%)
  matrix products  28.4 us (16%)
  other arithmetic  17 us (9%)
  between operations  14.2 us (8%)
  starting transfers between devices  4.3 us (2%)
  local copies, waits for them, and re-layouts  2.59 us (1%)
    psum x1, waiting for transfers between devices, block_step(): summed = lax.psum(partial_out, ('tp', 'sp'))  98.1 us
    dot_general x1, matrix products, local_partials(): jnp.einsum('bd,dkc->bkc', normed, w_qkv, preferred_element_type=jnp.float32)  18.4 us
    all_to_all x1, waiting for transfers between devices, block_step(): lax.all_to_all(packed.reshape(num_seqs, sp_size, head_share, width), 'sp'...  14.2 us
    select_n x1, other arithmetic, local_partials(): k_out = jnp.where(is_new, k_new[:, None], k_cache)  7.86 us
    dot_general x1, matrix products, block_step(): jnp.dot(combined.astype(jnp.bfloat16).reshape(num_seqs, head_share * head...  6.31 us
    all_to_all x1, starting transfers between devices, block_step(): lax.all_to_all(packed.reshape(num_seqs, sp_size, head_share, width), 'sp'...  4.3 us
  transfers between devices with their start and end apart: 2, of which 2 were waited for; matrix products, arithmetic and copies ran while one was open for 0% of the time, Pallas kernels for 0%

commit v1 on v0

v1 whole, which is shorter than its diff:
```python
import functools

import jax
import jax.numpy as jnp
from jax import lax
from jax.experimental import pallas as pl
from jax.experimental.pallas import tpu as pltpu
from jax.sharding import PartitionSpec as P

NORM_EPS = 1e-5
MESH = pl.DeviceIdType.MESH
F32 = jnp.float32
BF16 = jnp.bfloat16
VMEM = pltpu.VMEM
DMA = pltpu.SemaphoreType.DMA

B = 64
D = 8192
L = 64
HD = 128
G = 8
RD = 256
NB = D // RD
NC = 4
CB = B // NC
CR = CB * G
NSUB = 2
QW = 2048
UW = QW // NSUB
NU = NC * NSUB


def core_peer(sp):
    return sp + 1 - 2 * lax.rem(sp, 2)


def qkv_kernel(hid_ref, gain_ref, w_ref, b_ref, cos_ref, sin_ref, q_ref, kv_ref, wbuf, xexp, tot, wsem, ssem, rsem):
    sp = lax.axis_index("sp")
    core = lax.rem(sp, 2)
    base = core * 5

    def wcopy(c, ct):
        return pltpu.make_async_copy(
            w_ref.at[pl.ds(pl.multiple_of(c * RD, RD), RD), base + ct], wbuf.at[c, ct], wsem.at[c, ct])

    def start(c, carry):
        for ct in range(5):
            wcopy(c, ct).start()
        return carry

    lax.fori_loop(0, NB, start, 0)
    barrier = pltpu.get_barrier_semaphore()
    pl.semaphore_signal(barrier, inc=1, device_id={"sp": core_peer(sp)}, device_id_type=MESH)

    sq = jnp.zeros((B, 128), F32)
    for k in range(8):
        x = hid_ref[:, k * 1024:(k + 1) * 1024].astype(F32)
        x = x * x
        for j in range(8):
            sq = sq + x[:, j * 128:(j + 1) * 128]
    inv = lax.rsqrt(jnp.sum(sq, axis=-1, keepdims=True) / D + NORM_EPS)

    row = lax.broadcasted_iota(jnp.int32, (128, 256), 0)
    lane = lax.broadcasted_iota(jnp.int32, (128, 256), 1)
    spread = jnp.where(lax.div(lane, 2) == row, 1.0, 0.0).astype(BF16)
    even = lax.rem(lax.broadcasted_iota(jnp.int32, (B, 256), 1), 2) == 0

    def expand(k, carry):
        cols = pl.ds(pl.multiple_of(k * 128, 128), 128)
        wide = pl.ds(pl.multiple_of(k * 256, 256), 256)
        h = (hid_ref[:, cols].astype(F32) * inv * gain_ref[:, cols].astype(F32)).astype(BF16)
        t = jnp.dot(h, spread, preferred_element_type=F32)
        xexp[:B, wide] = jnp.where(even, t, 0.0).astype(BF16)
        xexp[B:, wide] = jnp.where(even, 0.0, t).astype(BF16)
        return carry

    lax.fori_loop(0, D // 128, expand, 0, unroll=4)

    tot[pl.ds(base, 5)] = jnp.zeros((5, 2 * B, HD), F32)

    def block(c, carry):
        for ct in range(5):
            wcopy(c, ct).wait()
        w = jnp.concatenate([wbuf.at[c, ct].reshape(2 * RD, HD)[...] for ct in range(5)], axis=1)
        wide = pl.ds(pl.multiple_of(c * 2 * RD, 2 * RD), 2 * RD)
        r = jnp.dot(xexp[:, wide], w, preferred_element_type=F32)
        for ct in range(5):
            tot[base + ct] += r[:, ct * HD:(ct + 1) * HD]
        return carry

    lax.fori_loop(0, NB, block, 0)
    pl.semaphore_wait(barrier, 1)
    copy = pltpu.make_async_remote_copy(
        src_ref=tot.at[pl.ds(base, 5)], dst_ref=tot.at[pl.ds(base, 5)], send_sem=ssem, recv_sem=rsem,
        device_id={"sp": core_peer(sp)}, device_id_type=MESH)
    copy.start()
    cos, sin = cos_ref[...], sin_ref[...]
    cos2 = jnp.concatenate([cos, cos], axis=1)
    sin2 = jnp.concatenate([-sin, sin], axis=1)
    bias = b_ref[...].astype(F32)
    copy.wait()
    for ct in range(10):
        for h in range(2):
            t = tot[ct, h * B:(h + 1) * B, :] + bias[h:h + 1, ct * HD:(ct + 1) * HD]
            if ct < 9:
                t = t * cos2 + pltpu.roll(t, 64, 1) * sin2
            t = t.astype(BF16).astype(F32)
            if ct < G:
                q_ref[h, pl.ds(ct, B, stride=G), :] = t
            else:
                kv_ref[ct - G, h] = t


def attend_kernel(q_ref, kv_ref, kc_ref, vc_ref, len_ref, sink_ref, ko_ref, vo_ref, n_ref, kbuf, vbuf, isem, osem):
    sp = lax.axis_index("sp")

    def load(src, dst, which, i):
        s = pl.ds(i * CB, CB)
        return pltpu.make_async_copy(src.at[s], dst.at[s], isem.at[which, i])

    def save(src, dst, which, i):
        s = pl.ds(i * CB, CB)
        return pltpu.make_async_copy(src.at[s], dst.at[s], osem.at[which, i])

    for i in range(NC):
        load(kc_ref, kbuf, 0, i).start()
        load(vc_ref, vbuf, 1, i).start()

    sub = lax.broadcasted_iota(jnp.int32, (G, HD), 0)
    lane = lax.broadcasted_iota(jnp.int32, (G, HD), 1)
    pos = lax.div(lane, 2)
    par = lax.rem(lane, 2)
    sinks = []
    for h in range(2):
        t = jnp.zeros((G, HD), F32)
        for g in range(G):
            t = jnp.where(sub == g, sink_ref[h * G + g], t)
        sinks.append(t)
    eye = lax.broadcasted_iota(jnp.int32, (CR, HD), 0) == lax.broadcasted_iota(jnp.int32, (CR, HD), 1)
    scale = HD ** -0.5

    def chunk(i, carry):
        load(kc_ref, kbuf, 0, i).wait()
        load(vc_ref, vbuf, 1, i).wait()
        locs = []
        for j in range(CB):
            b = i * CB + j
            loc = len_ref[b] - sp * L
            locs.append(loc)

            @pl.when((loc >= 0) & (loc < L))
            def _():
                for which, buf in ((0, kbuf), (1, vbuf)):
                    pair = jnp.concatenate([kv_ref[which, 0, pl.ds(b, 1), :], kv_ref[which, 1, pl.ds(b, 1), :]], axis=0)
                    buf[b, loc] = pair.astype(BF16)

        save(kbuf, ko_ref, 0, i).start()
        save(vbuf, vo_ref, 1, i).start()
        s0, s1 = [], []
        for j in range(CB):
            b = i * CB + j
            rows = pl.ds(pl.multiple_of(b * G, G), G)
            q = jnp.concatenate([q_ref[0, rows, :], q_ref[1, rows, :]], axis=0).astype(BF16)
            k = kbuf.at[b].reshape(2 * L, HD)[...]
            s = lax.dot_general(q, k, (((1,), (1,)), ((), ())), preferred_element_type=F32) * scale
            seen = pos <= locs[j]
            s0.append(jnp.where(seen & (par == 0), s[:G], -jnp.inf))
            s1.append(jnp.where(seen & (par == 1), s[G:], -jnp.inf))
        es = []
        for h, parts in ((0, s0), (1, s1)):
            s = jnp.concatenate(parts, axis=0)
            m = jnp.maximum(jnp.max(s, axis=-1, keepdims=True), jnp.concatenate([sinks[h][:, :1]] * CB, axis=0))
            e = jnp.exp(s - m)
            z = jnp.sum(e, axis=-1, keepdims=True)
            es.append(e)
            mrow = jnp.sum(jnp.where(eye, m, 0.0), axis=0, keepdims=True)
            zrow = jnp.sum(jnp.where(eye, z, 0.0), axis=0, keepdims=True)
            n_ref[i, h, CR:, :] = jnp.concatenate([mrow, zrow, jnp.zeros((6, HD), F32)], axis=0)
        for j in range(CB):
            b = i * CB + j
            e = jnp.concatenate([es[0][j * G:(j + 1) * G], es[1][j * G:(j + 1) * G]], axis=0).astype(BF16)
            v = vbuf.at[b].reshape(2 * L, HD)[...]
            r = jnp.dot(e, v, preferred_element_type=F32)
            n_ref[i, 0, j * G:(j + 1) * G, :] = r[:G]
            n_ref[i, 1, j * G:(j + 1) * G, :] = r[G:]
        return carry

    lax.fori_loop(0, NC, chunk, 0)
    for i in range(NC):
        save(kbuf, ko_ref, 0, i).wait()
        save(vbuf, vo_ref, 1, i).wait()


def out_kernel(n_ref, hid_ref, wo_ref, bo_ref, sink_ref, y_ref, wo, r1, comb, r2, obuf, part, near, both, other, full,
               wsem, s1, q1, s2, q2, s3, q3, sn, qn, sm, qm, sf, qf, sy, qy, sc, qc, sd, qd):
    sp = lax.axis_index("sp")
    z = lax.axis_index("tp")
    core = lax.rem(sp, 2)
    peer = core_peer(sp)
    ypeer = lax.rem(sp + 2, 4)
    zpeer = z + 1 - 2 * lax.rem(z, 2)
    zmid = 3 - z
    middle = (z == 1) | (z == 2)
    end = (z == 0) | (z == 3)

    def wcopy(k):
        rows = pl.ds(k * 512, 512)
        return pltpu.make_async_copy(
            wo_ref.at[rows, pl.ds(pl.multiple_of(sp * QW, QW), QW)], wo.at[rows], wsem.at[k])

    for k in range(4):
        wcopy(k).start()
    barrier = pltpu.get_barrier_semaphore()
    pl.semaphore_signal(barrier, inc=1, device_id={"sp": peer}, device_id_type=MESH)
    pl.semaphore_signal(barrier, inc=1, device_id={"sp": ypeer}, device_id_type=MESH)
    pl.semaphore_signal(barrier, inc=1, device_id={"tp": zpeer}, device_id_type=MESH)

    @pl.when(middle)
    def _():
        pl.semaphore_signal(barrier, inc=1, device_id={"tp": zmid}, device_id_type=MESH)
        pl.semaphore_wait(barrier, 4)

    @pl.when(end)
    def _():
        pl.semaphore_wait(barrier, 3)

    def remote(src, dst, send, recv, axis, target):
        return pltpu.make_async_remote_copy(
            src_ref=src, dst_ref=dst, send_sem=send, recv_sem=recv, device_id={axis: target}, device_id_type=MESH)

    def c_swap(i):
        return remote(n_ref.at[i, 1 - core], r1.at[i], s1.at[i], q1.at[i], "sp", peer)

    def c_y(i):
        return remote(comb.at[i], r2.at[i], s2.at[i], q2.at[i], "sp", ypeer)

    def c_o(i):
        return remote(obuf.at[core, i], obuf.at[core, i], s3.at[i], q3.at[i], "sp", peer)

    def c_near(u):
        return remote(part.at[u], near.at[u], sn.at[u], qn.at[u], "tp", zpeer)

    def c_mid(u):
        return remote(both.at[u], other.at[u], sm.at[u], qm.at[u], "tp", zmid)

    def c_full(u):
        return remote(full.at[sp, u], full.at[sp, u], sf.at[u], qf.at[u], "tp", zpeer)

    def c_fy(u):
        return remote(full.at[sp, u], full.at[sp, u], sy.at[u], qy.at[u], "sp", ypeer)

    def c_fc(u):
        return remote(full.at[sp, u], full.at[sp, u], sc.at[u], qc.at[u], "sp", peer)

    def c_fd(u):
        return remote(full.at[ypeer, u], full.at[ypeer, u], sd.at[u], qd.at[u], "sp", peer)

    for i in range(NC):
        c_swap(i).start()

    eye = lax.broadcasted_iota(jnp.int32, (CR, HD), 0) == lax.broadcasted_iota(jnp.int32, (CR, HD), 1)

    def column(r):
        return jnp.sum(jnp.where(eye, r, 0.0), axis=-1, keepdims=True)

    lane = lax.broadcasted_iota(jnp.int32, (1, HD), 1)
    sink = jnp.zeros((1, HD), F32)
    for g in range(G):
        sink = jnp.where(lax.rem(lane, G) == g, sink_ref[core * G + g], sink)

    for i in range(NC):
        c_swap(i).wait_recv()
        m1, m2 = n_ref[i, core, CR:CR + 1, :], r1[i, CR:CR + 1, :]
        z1, z2 = n_ref[i, core, CR + 1:CR + 2, :], r1[i, CR + 1:CR + 2, :]
        m = jnp.maximum(m1, m2)
        a1, a2 = jnp.exp(m1 - m), jnp.exp(m2 - m)
        comb[i, :CR, :] = n_ref[i, core, :CR, :] * column(a1) + r1[i, :CR, :] * column(a2)
        comb[i, CR:, :] = jnp.concatenate([m, z1 * a1 + z2 * a2, jnp.zeros((6, HD), F32)], axis=0)
        c_y(i).start()

    def project(i):
        c_y(i).wait_recv()
        m1, m2 = comb[i, CR:CR + 1, :], r2[i, CR:CR + 1, :]
        z1, z2 = comb[i, CR + 1:CR + 2, :], r2[i, CR + 1:CR + 2, :]
        m = jnp.maximum(m1, m2)
        a1, a2 = jnp.exp(m1 - m), jnp.exp(m2 - m)
        den = z1 * a1 + z2 * a2 + jnp.exp(sink - m)
        o = comb[i, :CR, :] * column(a1 / den) + r2[i, :CR, :] * column(a2 / den)
        obuf[core, i] = o.astype(BF16).astype(F32)
        c_o(i).start()
        if i == 0:
            for k in range(4):
                wcopy(k).wait()
        c_o(i).wait_recv()
        lhs = jnp.concatenate(
            [obuf[h, i, pl.ds(g, CB, stride=G), :] for h in range(2) for g in range(G)], axis=1).astype(BF16)
        for s in range(NSUB):
            def tile(t, carry):
                cols = pl.ds(pl.multiple_of(s * UW + t * 256, 256), 256)
                part[i * NSUB + s, :, pl.ds(pl.multiple_of(t * 256, 256), 256)] = jnp.dot(
                    lhs, wo[:, cols], preferred_element_type=F32)
                return carry
            lax.fori_loop(0, UW // 256, tile, 0)

            @pl.when(end)
            def _():
                c_near(i * NSUB + s).start()

    def gather(u):
        c_fy(u).start()
        c_fc(u).start()

    def first(u):
        @pl.when(middle)
        def _():
            c_near(u).wait_recv()
            both[u] = part[u] + near[u]
            c_mid(u).start()

    def second(u):
        @pl.when(middle)
        def _():
            c_mid(u).wait_recv()
            full[sp, u] = both[u] + other[u]
            c_full(u).start()
            gather(u)

    def third(u):
        @pl.when(end)
        def _():
            c_full(u).wait_recv()
            gather(u)

    def fourth(u):
        c_fy(u).wait_recv()
        c_fd(u).start()

    def last(u):
        c_fc(u).wait_recv()
        c_fd(u).wait_recv()
        i, s = u // NSUB, u % NSUB
        for k in range(4):
            cols = pl.ds(k * QW + s * UW, UW)
            rows = pl.ds(i * CB, CB)
            y_ref[rows, cols] = (hid_ref[rows, cols].astype(F32) + full[k, u] + bo_ref[:, cols].astype(F32)).astype(BF16)

    stages = ((first, 2), (second, 4), (third, 5), (fourth, 6), (last, 8))
    for t in range(NU + 8):
        if t % NSUB == 0 and t < NU:
            project(t // NSUB)
        for stage, lag in stages:
            if 0 <= t - lag < NU:
                stage(t - lag)

    for i in range(NC):
        c_swap(i).wait_send()
        c_y(i).wait_send()
        c_o(i).wait_send()
    for u in range(NU):
        c_fy(u).wait_send()
        c_fc(u).wait_send()
        c_fd(u).wait_send()

    @pl.when(middle)
    def _():
        for u in range(NU):
            c_mid(u).wait_send()
            c_full(u).wait_send()

    @pl.when(end)
    def _():
        for u in range(NU):
            c_near(u).wait_send()


def vm():
    return pl.BlockSpec(memory_space=VMEM)


def anywhere():
    return pl.BlockSpec(memory_space=pl.ANY)


def smem():
    return pl.BlockSpec(memory_space=pltpu.SMEM)


def solution(mesh):
    cache_spec = P("dp", "sp", "tp", None)

    def step(hidden, seq_lens, rope_cos, rope_sin, k_cache, v_cache, norm_gain, w_qkv, b_qkv, sink_logits, w_o, b_o):
        w_tiles = w_qkv.reshape(D, 2, 10, HD).transpose(0, 2, 1, 3)
        q, kv = pl.pallas_call(
            qkv_kernel,
            name="qkv",
            out_shape=(jax.ShapeDtypeStruct((2, B * G, HD), F32), jax.ShapeDtypeStruct((2, 2, B, HD), F32)),
            in_specs=[vm(), vm(), anywhere(), vm(), vm(), vm()],
            out_specs=(vm(), vm()),
            scratch_shapes=[
                VMEM((NB, 5, RD, 2, HD), BF16), VMEM((2 * B, 2 * D), BF16), VMEM((10, 2 * B, HD), F32),
                DMA((NB, 5)), DMA, DMA],
            compiler_params=pltpu.CompilerParams(
                collective_id=0, has_side_effects=True, vmem_limit_bytes=40 * 2**20),
        )(hidden, norm_gain.reshape(1, D), w_tiles, b_qkv, rope_cos, rope_sin)
        k_out, v_out, num = pl.pallas_call(
            attend_kernel,
            name="attend",
            out_shape=(jax.ShapeDtypeStruct((B, L, 2, HD), BF16), jax.ShapeDtypeStruct((B, L, 2, HD), BF16),
                       jax.ShapeDtypeStruct((NC, 2, CR + 8, HD), F32)),
            in_specs=[vm(), vm(), anywhere(), anywhere(), smem(), smem()],
            out_specs=(anywhere(), anywhere(), vm()),
            scratch_shapes=[VMEM((B, L, 2, HD), BF16), VMEM((B, L, 2, HD), BF16), DMA((2, NC)), DMA((2, NC))],
            compiler_params=pltpu.CompilerParams(vmem_limit_bytes=24 * 2**20),
        )(q, kv, k_cache, v_cache, seq_lens, sink_logits)
        unit = (NU, CB, UW)
        out_hidden = pl.pallas_call(
            out_kernel,
            name="out",
            out_shape=jax.ShapeDtypeStruct((B, D), BF16),
            in_specs=[vm(), vm(), anywhere(), vm(), smem()],
            out_specs=vm(),
            scratch_shapes=[
                VMEM((2048, QW), BF16),
                VMEM((NC, CR + 8, HD), F32), VMEM((NC, CR + 8, HD), F32), VMEM((NC, CR + 8, HD), F32),
                VMEM((2, NC, CR, HD), F32),
                VMEM(unit, F32), VMEM(unit, F32), VMEM(unit, F32), VMEM(unit, F32), VMEM((4, *unit), F32),
                DMA((4,))] + [DMA((NC,))] * 6 + [DMA((NU,))] * 12,
            compiler_params=pltpu.CompilerParams(
                collective_id=1, has_side_effects=True, vmem_limit_bytes=32 * 2**20),
        )(num, hidden, w_o, b_o.reshape(1, D), sink_logits)
        return out_hidden, k_out, v_out

    return jax.shard_map(
        step, mesh=mesh,
        in_specs=(P("dp", None), P("dp"), P("dp", None), P("dp", None), cache_spec, cache_spec, P(None),
                  P(None, "tp", None), P("tp", None), P("tp"), P("tp", None), P(None)),
        out_specs=(P("dp", None), cache_spec, cache_spec), check_vma=False)
```

time: 179 us -> 76.7 us (0.43)
  waiting for transfers between devices: 112 us -> 0 us
  Pallas kernels: 0 us -> 69.7 us
  matrix products: 28.4 us -> 0 us
  other arithmetic: 17 us -> 0 us
  between operations: 14.2 us -> 0.71 us
  starting transfers between devices: 4.3 us -> 0 us
  local copies, waits for them, and re-layouts: 2.59 us -> 5.89 us
    psum x1 -> x0, waiting for transfers between devices: 98.1 us -> none  [block_step(): summed = lax.psum(partial_out, ('tp', 'sp'))]
    pallas_call x0 -> x3, Pallas kernels: none -> 69.7 us  [the longest x1 42.6 us: step(): pl.pallas_call(out_kernel, name='out', out_shape=jax.ShapeDtypeStruct((B,...]
    dot_general x4 -> x0, matrix products: 28.4 us -> none  [the longest x1 18.4 us: local_partials(): jnp.einsum('bd,dkc->bkc', normed, w_qkv, preferred_element_type=jnp.float32)]
    all_to_all x1 -> x0, waiting for transfers between devices: 14.2 us -> none  [block_step(): lax.all_to_all(packed.reshape(num_seqs, sp_size, head_share, width), 'sp'...]
    select_n x1 -> x0, other arithmetic: 7.86 us -> none  [local_partials(): k_out = jnp.where(is_new, k_new[:, None], k_cache)]
    all_to_all x1 -> x0, starting transfers between devices: 4.3 us -> none  [block_step(): lax.all_to_all(packed.reshape(num_seqs, sp_size, head_share, width), 'sp'...]
    convert_element_type x4 -> x0, other arithmetic: 4.24 us -> none  [the longest x1 2.82 us: block_step(): (hidden.astype(jnp.float32) + summed + b_o.astype(jnp.float32)).astype(jn...]
    unnamed x16 -> x17, local copies, waits for them, and re-layouts: 1.11 us -> 4.41 us
  transfers between devices with their start and end apart: 2 -> 0, of which waited for: 2 -> 0; matrix products, arithmetic and copies ran while one was open for 0% -> 0% of each run, Pallas kernels for 0% -> 0%
where the time goes in v1:
time: 76.7 us; the launch traced here: 76.3 us
  Pallas kernels  69.7 us (91%)
  local copies, waits for them, and re-layouts  5.89 us (8%)
    pallas_call x1, Pallas kernels, step(): pl.pallas_call(out_kernel, name='out', out_shape=jax.ShapeDtypeStruct((B,...  42.6 us
    pallas_call x1, Pallas kernels, step(): pl.pallas_call(qkv_kernel, name='qkv', out_shape=(jax.ShapeDtypeStruct((2...  22.1 us
    pallas_call x1, Pallas kernels, step(): pl.pallas_call(attend_kernel, name='attend', out_shape=(jax.ShapeDtypeStr...  4.92 us
    unnamed x17, local copies, waits for them, and re-layouts  4.41 us

profile of v1, /device:TPU:0, one launch (start us, length us, event | category | flops | bytes accessed | tf_op | source)
XLA Modules:
  0.0 76.3 jit_solution(17767214872265563108)
XLA Ops:
  0.6 0.7 reshape.15.gain_ref
  1.4 0.7 reshape.17.bo_ref
  2.1 0.0 copy-start
  2.1 1.2 %copy-done = bf16[64,8192]{1,0:T(8,128)(2,1)S(1)} copy-done((bf16[64,8192]{1,0:T(8,128)(2,1)S(1)}, bf16[64,8192]{1,0:T(8,128)(2,1)}, u32[]{:S(2)}) %copy-start) | copy-done | bytes 1048600
  3.3 0.0 copy-start.3
  3.3 0.8 copy-done.3
  4.1 0.0 copy-start.4
  4.1 0.8 copy-done.4
  4.9 0.0 copy-start.5
  4.9 0.7 copy-done.5
  5.5 0.0 copy-start.1
  5.5 0.0 copy-start.2
  5.6 0.0 copy-start.6
  5.6 0.0 copy-start.7
  5.6 22.1 %qkv.1 = (f32[2,512,128]{2,1,0:T(8,128)S(1)}, f32[2,2,64,128]{3,2,1,0:T(8,128)S(1)}) custom-call(bf16[64,8192]{1,0:T(8,128)(2,1)S(1)} %copy-done, bf16[1,8192]{1,0:T(2,128)(2,1)S(1)} %reshape.15.gain_ref, bf16[8192,10,2,128]{3,2,1,0:T(2,128)(2,1)} %bitcast.3, bf16[2,1280]{1,0:T(2,128)(2,1)S(1)} %copy-done.5, f32[64,64]{1,0:T(8,128)S(1)} %copy-done.3, ...), custom_call_target="tpu_custom_call" | custom-call | tf_op jit(solution)/shard_map/qkv/pallas_call | solution.py:393
  27.7 0.0 copy-done.1
  27.7 0.0 copy-done.2
  27.7 0.0 copy-done.6
  27.7 0.0 copy-done.7
  27.7 4.9 %attend.1 = (bf16[64,64,2,128]{3,2,1,0:T(2,128)(2,1)}, bf16[64,64,2,128]{3,2,1,0:T(2,128)(2,1)}, f32[4,2,136,128]{3,2,1,0:T(8,128)S(1)}) custom-call(f32[2,512,128]{2,1,0:T(8,128)S(1)} %get-tuple-element.8.q_ref, f32[2,2,64,128]{3,2,1,0:T(8,128)S(1)} %get-tuple-element.9.kv_ref, bf16[64,64,2,128]{3,2,1,0:T(2,128)(2,1)S(1)} %copy-done.1, ...), custom_call_target="tpu_custom_call" | custom-call | tf_op jit(solution)/shard_map/attend/pallas_call | solution.py:405
  32.7 42.6 %out.1 = bf16[64,8192]{1,0:T(8,128)(2,1)S(1)} custom-call(f32[4,2,136,128]{3,2,1,0:T(8,128)S(1)} %get-tuple-element.10.n_ref, bf16[64,8192]{1,0:T(8,128)(2,1)S(1)} %copy-done, bf16[2048,8192]{1,0:T(8,128)(2,1)} %wo_ref.1, bf16[1,8192]{1,0:T(2,128)(2,1)S(1)} %reshape.17.bo_ref, f32[16]{0:T(128)S(1)} %copy-done.6), custom_call_target="tpu_custom_call" | custom-call | tf_op jit(solution)/shard_map/out/pallas_call | solution.py:416
  75.3 1.0 %copy.16 = bf16[64,8192]{1,0:T(8,128)(2,1)} copy(bf16[64,8192]{1,0:T(8,128)(2,1)S(1)} %out.1) | data formatting | bytes 2097152
Async XLA Ops:
  2.1 1.2 %copy-start = (bf16[64,8192]{1,0:T(8,128)(2,1)S(1)}, bf16[64,8192]{1,0:T(8,128)(2,1)}, u32[]{:S(2)}) copy-start(bf16[64,8192]{1,0:T(8,128)(2,1)} %hid_ref.3) | copy-start | bytes 3145732
  3.3 0.8 copy-start.3
  4.1 0.8 copy-start.4
  4.9 0.7 copy-start.5
  5.5 22.2 %copy-start.1 = (bf16[64,64,2,128]{3,2,1,0:T(2,128)(2,1)S(1)}, bf16[64,64,2,128]{3,2,1,0:T(2,128)(2,1)}, u32[]{:S(2)}) copy-start(bf16[64,64,2,128]{3,2,1,0:T(2,128)(2,1)} %kc_ref.1) | copy-start | bytes 6291460
  5.5 22.2 %copy-start.2 = (bf16[64,64,2,128]{3,2,1,0:T(2,128)(2,1)S(1)}, bf16[64,64,2,128]{3,2,1,0:T(2,128)(2,1)}, u32[]{:S(2)}) copy-start(bf16[64,64,2,128]{3,2,1,0:T(2,128)(2,1)} %vc_ref.1) | copy-start | bytes 6291460
  5.6 22.2 %copy-start.6 = (f32[16]{0:T(128)S(1)}, f32[16]{0:T(128)}, u32[]{:S(2)}) copy-start(f32[16]{0:T(128)} %sink_ref.3) | copy-start | bytes 196
  5.6 22.2 %copy-start.7 = (s32[64]{0:T(128)S(1)}, s32[64]{0:T(128)}, u32[]{:S(2)}) copy-start(s32[64]{0:T(128)} %len_ref.1) | copy-start | bytes 772
